TPU v7x, 256 devices: a whole 4x4x8 slice. The times are simulated.
256 devices in a mesh: ctx: 64 (over y, z, core), head: 4 (over x).
Axes of the slice: x: 4, y: 4, z: 8, core: 2. Of those that a mesh axis runs over, the one named last changes fastest.
Arguments:
- block_order: int32 [128], replicated, may hold values from 0 to 127, as said below
- main_query: bfloat16 [8192, 36864], P('ctx', 'head'), may hold values from -256 to 256
- latent_key: bfloat16 [576, 8192], P(None, 'ctx'), may hold values from -24 to 24
- index_query: bfloat16 [8192, 32, 128], P('ctx', 'head'), may hold values from -64 to 64
- index_weight: bfloat16 [8192, 32], P('ctx', 'head'), may hold values from -0.6 to 0.6
- index_key: bfloat16 [128, 8192], P(None, 'ctx'), may hold values from -24 to 24
Outputs:
- row_loss: float32 [8192], P('ctx')
- grad_query: bfloat16 [8192, 32, 128], P('ctx', 'head')
- grad_weight: bfloat16 [8192, 32], P('ctx', 'head')
- grad_key: float32 [8192, 128], P(('ctx', 'head'))
Inputs may be any that keep to these rules, and one draw needn't show every extreme that they name: `block_order`: slots 2d and 2d+1 hold blocks s * 64 + c and s * 64 + 128 // 2 - 1 - c of one sequence s, for some c below 32, and every block appears once.
All inputs are finite; a program needn't handle non-finite values.
Results may differ from a plain program's by a relative error of at most 0.01.
Values may be sent and summed in bfloat16 or wider, within the bound.
No kernel may reach another device: no remote copies, remote signals or barrier semaphores. Data moves between devices by JAX's collectives and lax.ppermute only.
A program may use at most 128 MiB of HBM per device.

v0:
```python
import math

import jax
import jax.numpy as jnp
from jax import lax
from jax.sharding import Mesh
from jax.sharding import PartitionSpec as P

HM = 64
HEAD_QK = 192
SEQS = 2
CTX = ("ctx_0", "ctx_1", "ctx_2")
CTX_HEAD = ("ctx_0", "ctx_1", "ctx_2", "head")


masked_value = -1e30


def side_by_side(arrays, axis, dim, along):
    ends, at = ([], 0)
    for a in arrays[:-1]:
        at += a.shape[along]
        ends.append(at)
    both = jnp.concatenate(arrays, axis=along)
    return tuple(jnp.split(lax.all_gather(both, axis, axis=dim, tiled=True), ends, axis=along))


def in_one_piece(arrays, axis, split_dim, concat_dim, along):
    widths = [math.prod(a.shape[along:]) for a in arrays]
    both = jnp.concatenate(
        [a.reshape(*a.shape[:along], w) for a, w in zip(arrays, widths)], axis=along
    )
    whole = lax.all_to_all(both, axis, split_axis=split_dim, concat_axis=concat_dim, tiled=True)
    blocks = jnp.split(whole, [sum(widths[:k]) for k in range(1, len(widths))], axis=along)
    return tuple(
        (b.reshape(*whole.shape[:along], *a.shape[along:]) for a, b in zip(arrays, blocks))
    )


def sent_to_all(shard, axis):
    copies = jnp.broadcast_to(shard, (lax.axis_size(axis), *shard.shape))
    return lax.all_to_all(copies, axis, split_axis=0, concat_axis=0, tiled=True)


def in_order(blocks, dim):
    shape = list(blocks.shape[1:])
    shape[dim] *= blocks.shape[0]
    return jnp.moveaxis(blocks, 0, dim).reshape(shape)


def gather_directly(shard, axis, dim):
    blocks = sent_to_all(shard, axis)
    return in_order(blocks, dim)


def sum_in_order(blocks, axes, sequence):
    inside = blocks.shape[1:]
    blocks = blocks.reshape(*(lax.axis_size(a) for a in axes), *inside)
    blocks = jnp.moveaxis(blocks, sequence, range(len(axes))).reshape(-1, *inside)
    for k in sequence:
        blocks = lax.psum_scatter(blocks, axes[k], scatter_dimension=0, tiled=True)
    return blocks[0]


def split_up(shard, dim, peers):
    shape = shard.shape
    blocks = shard.reshape(*shape[:dim], peers, shape[dim] // peers, *shape[dim + 1 :])
    return jnp.moveaxis(blocks, dim, 0)


def summed_rows(shard, axes, sequence, dim):
    peers = lax.axis_size(axes)
    return sum_in_order(split_up(shard, dim, peers), axes, sequence)


def pick_group(head_count, row_count):
    row_limit = max(256, row_count)
    chosen = 1
    for candidate in range(1, head_count + 1):
        if head_count % candidate == 0 and candidate * row_count <= row_limit:
            chosen = candidate
    return chosen


def window_start(row_pos, length):
    return row_pos[0] // length * length


def causal_target(queries, row_pos, key_rows, length):
    row_count = queries.shape[0]
    head_count = queries.shape[1]
    start_at = window_start(row_pos, length)
    window = lax.dynamic_slice_in_dim(key_rows, start_at, length, 1)
    key_pos = start_at + lax.iota(jnp.int32, length)
    visible = key_pos[None, :] <= row_pos[:, None]
    group_size = pick_group(head_count, row_count)
    score_scale = 1.0 / math.sqrt(HEAD_QK)
    target = jnp.zeros((row_count, length), jnp.float32)
    for group_index in range(head_count // group_size):
        grouped = queries[:, group_index * group_size : (group_index + 1) * group_size, :]
        scores = (
            jnp.einsum("rhk,ks->hrs", grouped, window, preferred_element_type=jnp.float32)
            * score_scale
        )
        scores = jnp.where(visible[None], scores, masked_value)
        top_score = jnp.max(scores, axis=2, keepdims=True)
        raised = jnp.exp(scores - top_score)
        target = target + jnp.sum(raised / jnp.sum(raised, axis=2, keepdims=True), axis=0)
    return (target * (1.0 / HM), start_at)


def index_scores(index_rows, index_weights, row_pos, key_rows, length):
    row_count = index_rows.shape[0]
    head_count = index_rows.shape[1]
    start_at = window_start(row_pos, length)
    window = lax.dynamic_slice_in_dim(key_rows, start_at, length, 1)
    key_pos = start_at + lax.iota(jnp.int32, length)
    visible = key_pos[None, :] <= row_pos[:, None]
    weights = index_weights.astype(jnp.float32)
    group_size = pick_group(head_count, row_count)
    logits = jnp.zeros((row_count, length), jnp.float32)
    for group_index in range(head_count // group_size):
        lower = group_index * group_size
        upper = lower + group_size
        activation = jnp.einsum(
            "rjd,ds->rjs", index_rows[:, lower:upper, :], window, preferred_element_type=jnp.float32
        )
        logits = logits + jnp.sum(
            jnp.maximum(activation, 0.0) * weights[:, lower:upper, None], axis=1
        )
    return jnp.where(visible, logits, 0.0)


def index_backward(index_rows, index_weights, row_pos, key_rows, slope_window, length):
    row_count = index_rows.shape[0]
    head_count = index_rows.shape[1]
    head_width = index_rows.shape[2]
    start_at = window_start(row_pos, length)
    window = lax.dynamic_slice_in_dim(key_rows, start_at, length, 1)
    weights = index_weights.astype(jnp.float32)
    slope_float = slope_window.astype(jnp.float32)
    group_size = pick_group(head_count, row_count)
    rows_parts = []
    weight_parts = []
    window_grad = jnp.zeros((length, head_width), jnp.float32)
    for group_index in range(head_count // group_size):
        lower = group_index * group_size
        upper = lower + group_size
        group_rows = index_rows[:, lower:upper, :]
        activation = jnp.einsum(
            "rjd,ds->rjs", group_rows, window, preferred_element_type=jnp.float32
        )
        weight_parts.append(jnp.sum(slope_float[:, None, :] * jnp.maximum(activation, 0.0), axis=2))
        through = jnp.where(
            activation > 0.0, slope_float[:, None, :] * weights[:, lower:upper, None], 0.0
        ).astype(jnp.bfloat16)
        rows_parts.append(
            jnp.einsum("rjs,ds->rjd", through, window, preferred_element_type=jnp.float32)
        )
        window_grad = window_grad + jnp.einsum(
            "rjs,rjd->sd", through, group_rows, preferred_element_type=jnp.float32
        )
    return (
        jnp.concatenate(rows_parts, axis=1),
        jnp.concatenate(weight_parts, axis=1),
        window_grad,
        start_at,
    )


def forward_items(main_rows, index_rows, index_weights, positions, sorted_latent, sorted_index):
    row_count = main_rows.shape[1]
    key_width = sorted_latent.shape[0]
    head_count = main_rows.shape[2] // key_width
    length = sorted_latent.shape[1] // SEQS
    queries = main_rows[0].reshape(row_count, head_count, key_width)
    target, start_at = causal_target(queries, positions[0], sorted_latent, length)
    targets = [target]
    starts = [start_at]
    logits_all = [index_scores(index_rows[0], index_weights[0], positions[0], sorted_index, length)]
    return (jnp.stack(targets), jnp.stack(logits_all), jnp.stack(starts))


def backward_items(index_rows, index_weights, positions, sorted_index, slope_windows, key_grad):
    length = slope_windows.shape[2]
    grad_rows, grad_weights, window_grad, start_at = index_backward(
        index_rows[0], index_weights[0], positions[0], sorted_index, slope_windows[0], length
    )
    key_grad = lax.dynamic_update_slice_in_dim(key_grad, window_grad, start_at, 0)
    grads_rows = [grad_rows]
    grads_weights = [grad_weights]
    return (jnp.stack(grads_rows), jnp.stack(grads_weights), key_grad)


def row_softmax(target, logits, positions, starts):
    length = logits.shape[2]
    key_pos = starts[:, None, None] + lax.iota(jnp.int32, length)[None, None, :]
    visible = key_pos <= positions[:, :, None]
    masked = jnp.where(visible, logits, masked_value)
    top_logit = jnp.max(masked, axis=2)
    total_exp = jnp.sum(jnp.where(visible, jnp.exp(masked - top_logit[:, :, None]), 0.0), axis=2)
    log_total = top_logit + jnp.log(total_exp)
    row_loss = jnp.sum(target, axis=2) * log_total - jnp.sum(target * logits, axis=2)
    slopes = jnp.where(visible, jnp.exp(masked - log_total[:, :, None]) - target, 0.0).astype(
        jnp.bfloat16
    )
    return (row_loss, lax.optimization_barrier(slopes))


def rows_work(
    main_rows, index_rows, index_weights, positions, sorted_latent, sorted_index, key_grad
):
    target, logits, starts = forward_items(
        main_rows, index_rows, index_weights, positions, sorted_latent, sorted_index
    )
    row_loss, slopes = row_softmax(target, logits, positions, starts)
    grad_rows, grad_weights, key_grad = backward_items(
        index_rows, index_weights, positions, sorted_index, slopes, key_grad
    )
    return (row_loss, grad_rows.astype(jnp.bfloat16), grad_weights.astype(jnp.bfloat16), key_grad)


def body(block_order, main_query, latent_key, index_query, index_weight, index_key):
    ctx_count = lax.axis_size(CTX)
    head_axis = lax.axis_size("head")
    local_rows = main_query.shape[0]
    block_rows = local_rows // 2
    seq_len = local_rows * ctx_count
    block_total = 2 * ctx_count
    key_width = latent_key.shape[0]
    index_width = index_key.shape[0]
    my_blocks = lax.dynamic_slice_in_dim(block_order, 2 * lax.axis_index(CTX), 2, 0)
    slot_of = jnp.argsort(block_order)
    local_pos = my_blocks[:, None] * block_rows + lax.iota(jnp.int32, block_rows)[None, :]
    all_latent, all_index = side_by_side((latent_key, index_key), CTX, 1, 0)
    sorted_latent = all_latent.reshape(key_width, block_total, block_rows)[:, slot_of, :].reshape(
        key_width, seq_len
    )
    sorted_index = all_index.reshape(index_width, block_total, block_rows)[:, slot_of, :].reshape(
        index_width, seq_len
    )
    key_grad = jnp.zeros((seq_len, index_width), jnp.float32)
    main_rows, index_rows, index_weights = (
        lax.all_to_all(main_query, "head", split_axis=0, concat_axis=1, tiled=True),
        *in_one_piece((index_query, index_weight), "head", 0, 1, 2),
    )
    part_rows = local_rows // head_axis
    positions = lax.dynamic_slice_in_dim(
        local_pos.reshape(local_rows), lax.axis_index("head") * part_rows, part_rows, 0
    )[None, :]
    row_loss, grad_rows, grad_weights, key_grad = rows_work(
        main_rows[None],
        index_rows[None],
        index_weights[None],
        positions,
        sorted_latent,
        sorted_index,
        key_grad,
    )
    grad_query, grad_weight = in_one_piece((grad_rows[0], grad_weights[0]), "head", 1, 0, 2)
    loss_rows = gather_directly(row_loss[0], "head", 0)
    stored_grad = key_grad.reshape(block_total, block_rows, index_width)[block_order].reshape(
        seq_len, index_width
    )
    grad_key = summed_rows(stored_grad.astype(jnp.bfloat16), CTX_HEAD, (2, 0, 1, 3), 0).astype(
        jnp.float32
    )
    return (loss_rows, grad_query, grad_weight, grad_key)


def solution(mesh):
    split = Mesh(
        mesh.devices.reshape(4, 8, 2, mesh.shape["head"]), ("ctx_0", "ctx_1", "ctx_2", "head")
    )
    in_specs = (
        P(),
        P(CTX, "head"),
        P(None, CTX),
        P(CTX, "head", None),
        P(CTX, "head"),
        P(None, CTX),
    )
    out_specs = (P(CTX), P(CTX, "head", None), P(CTX, "head"), P(CTX_HEAD, None))
    return jax.shard_map(body, mesh=split, in_specs=in_specs, out_specs=out_specs, check_vma=False)
```

profile of v0, /device:TPU:8, one launch (start us, length us, event | category | flops | bytes accessed | tf_op | source)
XLA Modules:
  0.0 366.5 jit_solution(10022678774724466950)
XLA Ops:
  12.7 4.3 %all-to-all-start.1 = ((bf16[128,8,129]{2,1,0:T(8,128)(2,1)}), bf16[128,8,129]{2,1,0:T(8,128)(2,1)S(1)}, u32[]{:S(2)}, u32[]{:S(2)}) async-start(bf16[128,8,129]{2,1,0:T(8,128)(2,1)} %pad_maximum_fusion), calls=%async_computation.1 | async-start | bytes 1048576 | tf_op jit(solution)/shard_map/all_to_all | solution.py:33
  21.4 5.1 %all-to-all-done.1 = bf16[128,8,129]{2,1,0:T(8,128)(2,1)S(1)} async-done(((bf16[128,8,129]{2,1,0:T(8,128)(2,1)}), bf16[128,8,129]{2,1,0:T(8,128)(2,1)S(1)}, u32[]{:S(2)}, u32[]{:S(2)}) %all-to-all-start.1) | async-done | bytes 264224 | tf_op jit(solution)/shard_map/all_to_all | solution.py:33
  26.5 3.6 all-to-all-start
  33.0 25.1 %all-to-all-done = bf16[4,32,9216]{2,1,0:T(8,128)(2,1)S(1)} async-done(((bf16[4,32,9216]{2,1,0:T(8,128)(2,1)}), bf16[4,32,9216]{2,1,0:T(8,128)(2,1)S(1)}, u32[]{:S(2)}, u32[]{:S(2)}) %all-to-all-start) | async-done | bytes 2359328 | tf_op jit(solution)/shard_map/all_to_all | solution.py:244
  61.4 4.6 %reshape_squeeze_broadcast_in_dim.3 = bf16[32,64,576]{2,1,0:T(8,128)(2,1)S(1)} reshape(bf16[32,4,9216]{2,1,0:T(4,128)(2,1)} %copy.131) | data formatting | bytes 4718592 | tf_op jit(solution)/shard_map/reshape;squeeze;broadcast_in_dim | solution.py:176
  67.2 35.2 %all-gather.2.cloned.1.call-done = bf16[704,8192]{0,1:T(8,128)(2,1)} async-done(((bf16[704,128]{0,1:T(8,128)(2,1)}), bf16[704,8192]{0,1:T(8,128)(2,1)}) %all-gather.2.cloned.1.call-update) | async-done | bytes 11534352 | tf_op jit(solution)/shard_map/all_gather | solution.py:25
  102.5 8.7 %split.21 = bf16[576,8192]{0,1:T(8,128)(2,1)} slice(bf16[704,8192]{0,1:T(8,128)(2,1)} %all-gather.2.cloned.1.call-done), slice={[0:576], [0:8192]} | slice | bytes 18874368 | tf_op jit(solution)/shard_map/split | solution.py:25
  111.2 12.2 %gather_fusion = bf16[128,576,64]{1,2,0:T(8,128)(2,1)} fusion(bf16[576,128,64]{0,2,1:T(8,128)(2,1)} %bitcast.173, s32[1024]{0:T(1024)S(1)} %pad_clamp_fusion.1), kind=kCustom, calls=%fused_computation | custom fusion | bytes 18874880 | tf_op jit(solution)/shard_map/gather | solution.py:236
  128.6 6.3 %fusion.25 = f32[8,32,4096]{2,1,0:T(8,128)} fusion(pred[32,4096]{1,0:T(8,128)(4,1)S(1)} %broadcast_compare_fusion, bf16[576,8192]{0,1:T(8,128)(2,1)} %bitcast.174, s32[]{:T(128)S(6)} %select_n.133, bf16[32,8,576]{2,1,0:T(8,128)(2,1)S(1)} %copy-done.24), kind=kOutput, calls=%fused_computation.29 | convolution fusion | flops 1210056704 | bytes 9863172 | tf_op jit(solution)/shard_map/rhk,ks->hrs/dot_general | solution.py:102
  135.0 5.7 %fusion.206 = f32[32,4096]{1,0:T(8,128)} fusion(f32[8,32,4096]{2,1,0:T(8,128)} %fusion.25), kind=kOutput, calls=%fused_computation.271 | output fusion | flops 3023358 | bytes 4718592 | tf_op jit(solution)/shard_map/div | solution.py:108
  140.6 6.3 %fusion.27 = f32[8,32,4096]{2,1,0:T(8,128)} fusion(pred[32,4096]{1,0:T(8,128)(4,1)S(1)} %broadcast_compare_fusion, bf16[576,8192]{0,1:T(8,128)(2,1)} %bitcast.175, s32[]{:T(128)S(6)} %select_n.133, bf16[32,8,576]{2,1,0:T(8,128)(2,1)S(1)} %copy-done.23), kind=kOutput, calls=%fused_computation.32 | convolution fusion | flops 1210056704 | bytes 9863172 | tf_op jit(solution)/shard_map/rhk,ks->hrs/dot_general | solution.py:102
  146.9 5.7 %fusion.207 = f32[32,4096]{1,0:T(8,128)} fusion(f32[8,32,4096]{2,1,0:T(8,128)} %fusion.27), kind=kOutput, calls=%fused_computation.272 | output fusion | flops 3023358 | bytes 4718592 | tf_op jit(solution)/shard_map/div | solution.py:108
  152.6 6.3 %fusion.29 = f32[8,32,4096]{2,1,0:T(8,128)} fusion(pred[32,4096]{1,0:T(8,128)(4,1)S(1)} %broadcast_compare_fusion, bf16[576,8192]{0,1:T(8,128)(2,1)} %bitcast.176, s32[]{:T(128)S(6)} %select_n.133, bf16[32,8,576]{2,1,0:T(8,128)(2,1)S(1)} %copy-done.22), kind=kOutput, calls=%fused_computation.35 | convolution fusion | flops 1210056704 | bytes 9863172 | tf_op jit(solution)/shard_map/rhk,ks->hrs/dot_general | solution.py:102
  158.9 5.6 %fusion.208 = f32[32,4096]{1,0:T(8,128)} fusion(f32[8,32,4096]{2,1,0:T(8,128)} %fusion.29), kind=kOutput, calls=%fused_computation.273 | output fusion | flops 3023358 | bytes 4718592 | tf_op jit(solution)/shard_map/div | solution.py:108
  164.6 6.3 %fusion.31 = f32[8,32,4096]{2,1,0:T(8,128)} fusion(pred[32,4096]{1,0:T(8,128)(4,1)S(1)} %broadcast_compare_fusion, bf16[576,8192]{0,1:T(8,128)(2,1)} %bitcast.177, s32[]{:T(128)S(6)} %select_n.133, bf16[32,8,576]{2,1,0:T(8,128)(2,1)S(1)} %copy-done.21), kind=kOutput, calls=%fused_computation.38 | convolution fusion | flops 1210056704 | bytes 9863172 | tf_op jit(solution)/shard_map/rhk,ks->hrs/dot_general | solution.py:102
  170.9 5.8 %fusion.209 = f32[32,4096]{1,0:T(8,128)} fusion(f32[8,32,4096]{2,1,0:T(8,128)} %fusion.31), kind=kOutput, calls=%fused_computation.274 | output fusion | flops 3023358 | bytes 4718592 | tf_op jit(solution)/shard_map/div | solution.py:108
  176.7 6.3 %fusion.33 = f32[8,32,4096]{2,1,0:T(8,128)} fusion(pred[32,4096]{1,0:T(8,128)(4,1)S(1)} %broadcast_compare_fusion, bf16[576,8192]{0,1:T(8,128)(2,1)} %bitcast.178, s32[]{:T(128)S(6)} %select_n.133, bf16[32,8,576]{2,1,0:T(8,128)(2,1)S(1)} %copy-done.20), kind=kOutput, calls=%fused_computation.41 | convolution fusion | flops 1210056704 | bytes 9863172 | tf_op jit(solution)/shard_map/rhk,ks->hrs/dot_general | solution.py:102
  183.0 5.7 %fusion.210 = f32[32,4096]{1,0:T(8,128)} fusion(f32[8,32,4096]{2,1,0:T(8,128)} %fusion.33), kind=kOutput, calls=%fused_computation.275 | output fusion | flops 3023358 | bytes 4718592 | tf_op jit(solution)/shard_map/div | solution.py:108
  188.7 6.3 %fusion.35 = f32[8,32,4096]{2,1,0:T(8,128)} fusion(pred[32,4096]{1,0:T(8,128)(4,1)S(1)} %broadcast_compare_fusion, bf16[576,8192]{0,1:T(8,128)(2,1)} %bitcast.179, s32[]{:T(128)S(6)} %select_n.133, bf16[32,8,576]{2,1,0:T(8,128)(2,1)S(1)} %copy-done.19), kind=kOutput, calls=%fused_computation.44 | convolution fusion | flops 1210056704 | bytes 9863172 | tf_op jit(solution)/shard_map/rhk,ks->hrs/dot_general | solution.py:102
  195.1 5.8 %fusion.211 = f32[32,4096]{1,0:T(8,128)} fusion(f32[8,32,4096]{2,1,0:T(8,128)} %fusion.35), kind=kOutput, calls=%fused_computation.276 | output fusion | flops 3023358 | bytes 4718592 | tf_op jit(solution)/shard_map/div | solution.py:108
  200.9 6.5 %fusion.37 = f32[8,32,4096]{2,1,0:T(8,128)} fusion(pred[32,4096]{1,0:T(8,128)(4,1)S(1)} %broadcast_compare_fusion, bf16[576,8192]{0,1:T(8,128)(2,1)} %bitcast.180, s32[]{:T(128)S(6)} %select_n.133, bf16[32,8,576]{2,1,0:T(8,128)(2,1)S(1)} %get-tuple-element.24), kind=kOutput, calls=%fused_computation.47 | convolution fusion | flops 1210056704 | bytes 9863172 | tf_op jit(solution)/shard_map/rhk,ks->hrs/dot_general | solution.py:102
  207.4 3.9 %fusion.39 = f32[8,32,4096]{2,1,0:T(8,128)} fusion(pred[32,4096]{1,0:T(8,128)(4,1)S(1)} %broadcast_compare_fusion, bf16[576,8192]{0,1:T(8,128)(2,1)S(1)} %bitcast.183, s32[]{:T(128)S(6)} %select_n.133, bf16[32,8,576]{2,1,0:T(8,128)(2,1)S(1)} %get-tuple-element.30), kind=kOutput, calls=%fused_computation.50 | convolution fusion | flops 1210056704 | bytes 9895940 | tf_op jit(solution)/shard_map/rhk,ks->hrs/dot_general | solution.py:102
  211.3 5.6 %fusion.212 = f32[32,4096]{1,0:T(8,128)} fusion(f32[8,32,4096]{2,1,0:T(8,128)} %fusion.39), kind=kOutput, calls=%fused_computation.277 | output fusion | flops 3023358 | bytes 4718592 | tf_op jit(solution)/shard_map/div | solution.py:108
  216.9 5.8 %fusion.213 = f32[32,4096]{1,0:T(8,128)} fusion(f32[8,32,4096]{2,1,0:T(8,128)} %fusion.37), kind=kOutput, calls=%fused_computation.278 | output fusion | flops 3023358 | bytes 4718592 | tf_op jit(solution)/shard_map/div | solution.py:108
  243.5 3.9 %gather_fusion.2 = bf16[128,64,128]{2,1,0:T(8,128)(2,1)} fusion(bf16[128,64,128]{2,1,0:T(8,128)(2,1)} %bitcast.40, s32[1024]{0:T(1024)} %pad_clamp_fusion), kind=kCustom, calls=%fused_computation.2 | custom fusion | bytes 4194816 | tf_op jit(solution)/shard_map/gather | solution.py:262
  252.9 11.6 %reduce-scatter.5.cloned.1.call-done = bf16[128,32,128]{2,1,0:T(8,128)(2,1)} async-done(((bf16[256,32,128]{2,1,0:T(8,128)(2,1)}), bf16[128,32,128]{2,1,0:T(8,128)(2,1)}) %reduce-scatter.5.cloned.1.call-update) | async-done | bytes 1048592 | tf_op jit(solution)/shard_map/reduce_scatter | solution.py:61
  265.9 4.3 %all-to-all-start.2 = ((f32[4,1,32]{2,1,0:T(1,128)}), f32[4,1,32]{2,1,0:T(1,128)S(1)}, u32[]{:S(2)}, u32[]{:S(2)}) async-start(f32[4,1,32]{2,1,0:T(1,128)} %broadcast_in_dim.123), calls=%async_computation.2 | async-start | bytes 4096 | tf_op jit(solution)/shard_map/all_to_all | solution.py:42
  270.1 6.8 %multiply_reduce_fusion.3 = (bf16[32,8]{1,0:T(8,128)(2,1)S(1)}, bf16[32,8]{1,0:T(8,128)(2,1)S(1)}, bf16[32,8]{1,0:T(8,128)(2,1)S(1)}, bf16[32,8]{1,0:T(8,128)(2,1)S(1)}) fusion(f32[32,8,4096]{2,1,0:T(8,128)} %copy-done.3, f32[32,4096]{1,0:T(8,128)S(1)} %copy-done.8, f32[32,8,4096]{2,1,0:T(8,128)} %copy-done.2, f32[32,8,4096]{2,1,0:T(8,128)} %copy-done.1, ...), kind=kLoop, calls=%fused_computation.95 | loop fusion | flops 12581888 | bytes 17303552 | tf_op jit(solution)/shard_map/reduce_sum | solution.py:153
  280.2 12.2 %reduce-scatter.7.cloned.1.call-done = bf16[32,32,128]{2,1,0:T(8,128)(2,1)} async-done(((bf16[128,32,128]{2,1,0:T(8,128)(2,1)}), bf16[32,32,128]{2,1,0:T(8,128)(2,1)}) %reduce-scatter.7.cloned.1.call-update) | async-done | bytes 262160 | tf_op jit(solution)/shard_map/reduce_scatter | solution.py:61
  294.4 4.3 %all-to-all-start.3 = ((bf16[32,32,129]{2,0,1:T(8,128)(2,1)}), bf16[32,32,129]{2,0,1:T(8,128)(2,1)S(1)}, u32[]{:S(2)}, u32[]{:S(2)}) async-start(bf16[32,32,129]{2,0,1:T(8,128)(2,1)} %copy.151), calls=%async_computation.3 | async-start | bytes 1048576 | tf_op jit(solution)/shard_map/all_to_all | solution.py:33
  298.8 35.4 %reduce-scatter.9.cloned.1.call-done = bf16[4,32,128]{2,1,0:T(8,128)(2,1)} async-done(((bf16[32,32,128]{2,1,0:T(8,128)(2,1)}), bf16[4,32,128]{2,1,0:T(8,128)(2,1)}) %reduce-scatter.9.cloned.1.call-update) | async-done | bytes 32784 | tf_op jit(solution)/shard_map/reduce_scatter | solution.py:61
  337.7 20.5 %reduce-scatter.11.cloned.1.call-done = bf16[1,32,128]{2,1,0:T(8,128)(2,1)} async-done(((bf16[4,32,128]{2,1,0:T(8,128)(2,1)}), bf16[1,32,128]{2,1,0:T(8,128)(2,1)}) %reduce-scatter.11.cloned.1.call-update) | async-done | bytes 8208 | tf_op jit(solution)/shard_map/reduce_scatter | solution.py:61
  (167 shorter events, 59.8 us)
Async XLA Ops:
  7.2 23.0 %copy-start.39 = (s32[128]{0:T(128)S(1)}, s32[128]{0:T(128)}, u32[]{:S(2)}) copy-start(s32[128]{0:T(128)} %param.6) | copy-start | bytes 1540
  7.2 95.3 %all-gather.2.cloned.1.call-start = ((), (), s32[]{:S(2)}) async-start(), calls=%async_computation.8 | async-start | bytes 12779520 | tf_op jit(solution)/shard_map/all_gather | solution.py:25
  12.7 13.8 %all-to-all-start.1 = ((bf16[128,8,129]{2,1,0:T(8,128)(2,1)}), bf16[128,8,129]{2,1,0:T(8,128)(2,1)S(1)}, u32[]{:S(2)}, u32[]{:S(2)}) async-start(bf16[128,8,129]{2,1,0:T(8,128)(2,1)} %pad_maximum_fusion), calls=%async_computation.1 | async-start | bytes 1048576 | tf_op jit(solution)/shard_map/all_to_all | solution.py:33
  18.0 43.4 %copy-start.36 = (s32[32]{0:T(128)}, s32[32]{0:T(128)S(1)}, u32[]{:S(2)}) copy-start(s32[32]{0:T(128)S(1)} %dynamic_slice.14) | copy-start | bytes 388
  26.5 31.6 %all-to-all-start = ((bf16[4,32,9216]{2,1,0:T(8,128)(2,1)}), bf16[4,32,9216]{2,1,0:T(8,128)(2,1)S(1)}, u32[]{:S(2)}, u32[]{:S(2)}) async-start(bf16[4,32,9216]{2,1,0:T(8,128)(2,1)} %bitcast.196), calls=%async_computation | async-start | bytes 4718592 | tf_op jit(solution)/shard_map/all_to_all | solution.py:244
  30.1 234.4 %reduce-scatter.5.cloned.1.call-start = ((), (), s32[]{:S(2)}) async-start(), calls=%async_computation.9 | async-start | bytes 3145728 | tf_op jit(solution)/shard_map/reduce_scatter | solution.py:61
  134.9 5.7 %copy-start.23 = (bf16[32,8,576]{2,1,0:T(8,128)(2,1)S(1)}, bf16[32,8,576]{2,1,0:T(8,128)(2,1)}, u32[]{:S(2)}) copy-start(bf16[32,8,576]{2,1,0:T(8,128)(2,1)} %get-tuple-element.25) | copy-start | bytes 884740
  146.9 5.7 %copy-start.22 = (bf16[32,8,576]{2,1,0:T(8,128)(2,1)S(1)}, bf16[32,8,576]{2,1,0:T(8,128)(2,1)}, u32[]{:S(2)}) copy-start(bf16[32,8,576]{2,1,0:T(8,128)(2,1)} %get-tuple-element.26) | copy-start | bytes 884740
  158.9 5.6 %copy-start.21 = (bf16[32,8,576]{2,1,0:T(8,128)(2,1)S(1)}, bf16[32,8,576]{2,1,0:T(8,128)(2,1)}, u32[]{:S(2)}) copy-start(bf16[32,8,576]{2,1,0:T(8,128)(2,1)} %get-tuple-element.27) | copy-start | bytes 884740
  170.9 5.8 %copy-start.20 = (bf16[32,8,576]{2,1,0:T(8,128)(2,1)S(1)}, bf16[32,8,576]{2,1,0:T(8,128)(2,1)}, u32[]{:S(2)}) copy-start(bf16[32,8,576]{2,1,0:T(8,128)(2,1)} %get-tuple-element.28) | copy-start | bytes 884740
  183.0 5.7 %copy-start.19 = (bf16[32,8,576]{2,1,0:T(8,128)(2,1)S(1)}, bf16[32,8,576]{2,1,0:T(8,128)(2,1)}, u32[]{:S(2)}) copy-start(bf16[32,8,576]{2,1,0:T(8,128)(2,1)} %get-tuple-element.29) | copy-start | bytes 884740
  195.1 12.3 %slice-start = ((s8[10485760]{0:T(1024)(128)(4,1)}), s8[2097152]{0:T(1024)(128)(4,1)S(1)}, s32[]{:S(2)}) async-start(s8[10485760]{0:T(1024)(128)(4,1)} %bitcast.181), calls=%async_computation.13 | async-start | bytes 4194304
  200.9 6.5 %slice-start.1 = ((s8[10485760]{0:T(1024)(128)(4,1)}), s8[4194304]{0:T(1024)(128)(4,1)S(1)}, s32[]{:S(2)}) async-start(s8[10485760]{0:T(1024)(128)(4,1)} %bitcast.181), calls=%async_computation.14 | async-start | bytes 8388608
  200.9 6.5 %slice-start.2 = ((s8[10485760]{0:T(1024)(128)(4,1)}), s8[4194304]{0:T(1024)(128)(4,1)S(1)}, s32[]{:S(2)}) async-start(s8[10485760]{0:T(1024)(128)(4,1)} %bitcast.181), calls=%async_computation.15 | async-start | bytes 8388608
  216.9 5.8 %copy-start.4 = (bf16[128,128,64]{1,2,0:T(8,128)(2,1)S(1)}, bf16[128,128,64]{1,2,0:T(8,128)(2,1)}, u32[]{:S(2)}) copy-start(bf16[128,128,64]{1,2,0:T(8,128)(2,1)} %gather_fusion.1) | copy-start | bytes 6291460
  216.9 5.8 %copy-start.6 = (bf16[4,32,8,129]{3,2,0,1:T(8,128)(2,1)S(1)}, bf16[4,32,8,129]{3,2,0,1:T(8,128)(2,1)}, u32[]{:S(2)}) copy-start(bf16[4,32,8,129]{3,2,0,1:T(8,128)(2,1)} %copy-done.5) | copy-start | bytes 792580
  216.9 5.8 %copy-start.29 = (f32[32,8]{1,0:T(8,128)S(1)}, f32[32,8]{1,0:T(8,128)}, u32[]{:S(2)}) copy-start(f32[32,8]{1,0:T(8,128)} %get-tuple-element.33) | copy-start | bytes 3076
  229.5 3.1 copy-start.16
  229.5 3.6 copy-start.17
  229.5 4.1 %copy-start.18 = (f32[32,4096]{1,0:T(8,128)S(1)}, f32[32,4096]{1,0:T(8,128)}, u32[]{:S(2)}) copy-start(f32[32,4096]{1,0:T(8,128)} %fusion.213) | copy-start | bytes 1572868
  231.1 3.8 %copy-start.3 = (f32[32,8,4096]{2,1,0:T(8,128)}, f32[32,8,4096]{2,1,0:T(8,128)S(1)}, u32[]{:S(2)}) copy-start(f32[32,8,4096]{2,1,0:T(8,128)S(1)} %get-tuple-element.41) | copy-start | bytes 12582916
  235.5 5.7 %copy-start.7 = (f32[32,4096]{1,0:T(8,128)}, f32[32,4096]{1,0:T(8,128)S(1)}, u32[]{:S(2)}) copy-start(f32[32,4096]{1,0:T(8,128)S(1)} %bitcast_convert_fusion) | copy-start | bytes 1572868
  238.1 3.1 copy-start.30
  247.4 22.7 %copy-start.8 = (f32[32,4096]{1,0:T(8,128)S(1)}, f32[32,4096]{1,0:T(8,128)}, u32[]{:S(2)}) copy-start(f32[32,4096]{1,0:T(8,128)} %copy-done.7) | copy-start | bytes 1572868
  251.1 41.4 %reduce-scatter.7.cloned.1.call-start = ((), (), s32[]{:S(2)}) async-start(), calls=%async_computation.10 | async-start | bytes 1310720 | tf_op jit(solution)/shard_map/reduce_scatter | solution.py:61
  265.9 28.6 %all-to-all-start.2 = ((f32[4,1,32]{2,1,0:T(1,128)}), f32[4,1,32]{2,1,0:T(1,128)S(1)}, u32[]{:S(2)}, u32[]{:S(2)}) async-start(f32[4,1,32]{2,1,0:T(1,128)} %broadcast_in_dim.123), calls=%async_computation.2 | async-start | bytes 4096 | tf_op jit(solution)/shard_map/all_to_all | solution.py:42
  270.1 7.8 %copy-start.35 = (f32[32,8]{1,0:T(8,128)S(1)}, f32[32,8]{1,0:T(8,128)}, u32[]{:S(2)}) copy-start(f32[32,8]{1,0:T(8,128)} %get-tuple-element.32) | copy-start | bytes 3076
  270.1 64.0 %reduce-scatter.9.cloned.1.call-start = ((), (), s32[]{:S(2)}) async-start(), calls=%async_computation.11 | async-start | bytes 294912 | tf_op jit(solution)/shard_map/reduce_scatter | solution.py:61
  279.5 13.0 %copy-start.26 = (u32[8,4096]{1,0:T(8,128)S(1)}, u32[8,4096]{1,0:T(8,128)}, u32[]{:S(2)}) copy-start(u32[8,4096]{1,0:T(8,128)} %copy-done.25) | copy-start | bytes 393220
  279.5 13.0 %copy-start.28 = (f32[32,8]{1,0:T(8,128)S(1)}, f32[32,8]{1,0:T(8,128)}, u32[]{:S(2)}) copy-start(f32[32,8]{1,0:T(8,128)} %get-tuple-element.35) | copy-start | bytes 3076
  294.4 41.5 %all-to-all-start.3 = ((bf16[32,32,129]{2,0,1:T(8,128)(2,1)}), bf16[32,32,129]{2,0,1:T(8,128)(2,1)S(1)}, u32[]{:S(2)}, u32[]{:S(2)}) async-start(bf16[32,32,129]{2,0,1:T(8,128)(2,1)} %copy.151), calls=%async_computation.3 | async-start | bytes 1048576 | tf_op jit(solution)/shard_map/all_to_all | solution.py:33
  298.8 59.4 %reduce-scatter.11.cloned.1.call-start = ((), (), s32[]{:S(2)}) async-start(), calls=%async_computation.12 | async-start | bytes 40960 | tf_op jit(solution)/shard_map/reduce_scatter | solution.py:61
  (20 other events, 37.7 us)
Sparse Core Ops, SparseCore 0:
  11.3 91.1 all-gather.1
  251.2 13.3 reduce-scatter.4
  267.1 25.2 reduce-scatter.6
  294.8 39.2 reduce-scatter.8
  336.5 21.7 reduce-scatter.10
where the time goes:
time: 373 us; the launch traced here: 366 us
  waiting for transfers between devices  145 us (39%)
  other arithmetic  68.7 us (18%)
  matrix products  64.3 us (17%)
  local copies, waits for them, and re-layouts  56.6 us (15%)
  starting transfers between devices  16.6 us (4%)
  between operations  15 us (4%)
    reduce_scatter x4, waiting for transfers between devices, sum_in_order(): blocks = lax.psum_scatter(blocks, axes[k], scatter_dimension=0, tiled=True)  79.7 us
    dot_general x8, matrix products, causal_target(): jnp.einsum('rhk,ks->hrs', grouped, window, preferred_element_type=jnp.flo...  48.3 us
    div x8, other arithmetic, causal_target(): raised / jnp.sum(raised, axis=2, keepdims=True)  45.7 us
    all_gather x1, waiting for transfers between devices, side_by_side(): lax.all_gather(both, axis, axis=dim, tiled=True)  35.2 us
    all_to_all x1, waiting for transfers between devices, body(): lax.all_to_all(main_query, 'head', split_axis=0, concat_axis=1, tiled=True)  25.1 us
    gather x1, local copies, waits for them, and re-layouts, body(): all_latent.reshape(key_width, block_total, block_rows)[:, slot_of, :]  12.2 us
    split x2, local copies, waits for them, and re-layouts, side_by_side(): jnp.split(lax.all_gather(both, axis, axis=dim, tiled=True), ends, axis=al...  11.7 us
    all_to_all x2, starting transfers between devices, in_one_piece(): lax.all_to_all(both, axis, split_axis=split_dim, concat_axis=concat_dim,...  8.61 us
  transfers between devices with their start and end apart: 9, of which 7 were waited for; matrix products, arithmetic and copies ran while one was open for 10% of the time, Pallas kernels for 0%

commit v1 on v0

v1 whole, which is shorter than its diff:
```python
import math

import jax
import jax.numpy as jnp
from jax import lax
from jax.experimental import pallas as pl
from jax.experimental.pallas import tpu as pltpu
from jax.sharding import Mesh
from jax.sharding import PartitionSpec as P

HM = 64
HI = 32
DI = 128
KW = 576
HEAD_QK = 192
BLOCK = 64
LENGTH = 4096
HALF = LENGTH // 2
CTX = ("ctx_0", "ctx_1", "ctx_2")
CTX_HEAD = ("ctx_0", "ctx_1", "ctx_2", "head")
HEADS = 4
GROUP = 16
MAIN_LANES = HM // HEADS * KW
INDEX_LANES = HI // HEADS * DI
ALL_LANES = MAIN_LANES + INDEX_LANES + 128
TILE = 256
TILES = LENGTH // TILE
PAIRS = LENGTH // TILE
ROWS = HM * GROUP
IROWS = HI * GROUP
KEY_ROWS = 1024
GRAD_ROWS = 9 * 2 * GROUP
masked_value = -1e30
SCORE_EXP2 = math.log2(math.e) / math.sqrt(HEAD_QK)
f32 = jnp.float32
bf16 = jnp.bfloat16


def nt_dot(a, b):
    return lax.dot_general(a, b, (((1,), (1,)), ((), ())), preferred_element_type=f32)


def rows_kernel(
    where_ref, meta_ref, gathered, q_ref, out_ref,
    raw, keys, q_all, qi_all, scores, best, total, w_all, target, logits, slope, gsum, key_grad, sems,
):
    c_own = meta_ref[0]
    h_own = meta_ref[1]

    def fetch(n):
        return pltpu.make_async_copy(gathered.at[where_ref[n]], raw.at[n], sems.at[n])

    for n in range(32):
        fetch(n).start()

    keys[0:64, :] = jnp.zeros((64, LENGTH), bf16)
    keys[640:704, :] = jnp.zeros((64, LENGTH), bf16)

    for e in range(2):
        for src in range(HEADS):
            for i in range(8):
                at = (src * 8 + i) * GROUP
                for parity in range(2):
                    lane = i * 2 * KW + parity * (KW - 64)
                    q_all[e, parity, at : at + GROUP, :] = q_ref[src, e, :, lane : lane + 640]
                lane = MAIN_LANES + i * DI
                qi_all[e, at : at + GROUP, :] = q_ref[src, e, :, lane : lane + DI]
                lane = MAIN_LANES + INDEX_LANES
                column = q_ref[src, e, :, lane : lane + 128].astype(f32)[:, i : i + 1]
                w_all[e, at : at + GROUP, :] = jnp.broadcast_to(column, (GROUP, DI))

    take = lax.broadcasted_iota(jnp.int32, (256, 256), 0)
    give = lax.broadcasted_iota(jnp.int32, (256, 256), 1)
    source = jnp.where(give // 64 == 1, give + 64, jnp.where(give // 64 == 2, give - 64, give))
    shuffle = jnp.where(take == source, 1.0, 0.0).astype(bf16)

    def sort_pair(i, carry):
        fetch(2 * i).wait()
        fetch(2 * i + 1).wait()
        both = jnp.concatenate([raw[2 * i], raw[2 * i + 1]], axis=1)
        mixed = jnp.dot(both, shuffle, preferred_element_type=f32).astype(bf16)
        early = pl.multiple_of(i * 128, 128)
        late = pl.multiple_of(HALF + i * 128, 128)
        keys[64:640, pl.ds(early, 128)] = mixed[0:KW, 0:128]
        keys[704:832, pl.ds(early, 128)] = mixed[KW:, 0:128]
        keys[64:640, pl.ds(late, 128)] = mixed[0:KW, 128:256]
        keys[704:832, pl.ds(late, 128)] = mixed[KW:, 128:256]
        return carry

    lax.fori_loop(0, 16, sort_pair, 0)

    key_grad[...] = jnp.zeros((DI, LENGTH), f32)

    for e in range(2):
        row_pos = lax.broadcasted_iota(jnp.int32, (GROUP, 1), 0) + h_own * GROUP
        row_pos = row_pos + (c_own if e == 0 else 63 - c_own) * BLOCK

        def key_pos(at, width):
            lane = lax.broadcasted_iota(jnp.int32, (1, width), 1) + at
            late_lane = lane - HALF
            late_pos = (63 - late_lane // BLOCK) * BLOCK + late_lane % BLOCK
            return jnp.where(lane < HALF, lane, late_pos)

        early_tiles = c_own // 4 + 1 if e == 0 else TILES // 2
        late_tiles = 0 if e == 0 else TILES // 2 - c_own // 4

        def tile_at(j):
            if e == 0:
                return pl.multiple_of(j * TILE, TILE)
            return pl.multiple_of(jnp.where(j < TILES // 2, j, j + c_own // 4) * TILE, TILE)

        steps = early_tiles + late_tiles

        best[...] = jnp.full((ROWS, 128), masked_value, f32)
        total[...] = jnp.zeros((ROWS, 128), f32)
        target[...] = jnp.zeros((GROUP, LENGTH), f32)
        logits[...] = jnp.full((GROUP, LENGTH), masked_value, f32)

        def score_step(j, carry):
            at = tile_at(j)
            visible = key_pos(at, TILE) <= row_pos
            for parity in range(2):
                k = keys[64 * (1 - parity) : 64 * (1 - parity) + 640, pl.ds(at, TILE)]
                s = jnp.dot(q_all[e, parity], k, preferred_element_type=f32)
                s = jnp.where(visible[None], s.reshape(HM // 2, GROUP, TILE), masked_value)
                s = s.reshape(ROWS // 2, TILE)
                r = slice(parity * (ROWS // 2), (parity + 1) * (ROWS // 2))
                scores[r, pl.ds(at, TILE)] = s
                best[r] = jnp.maximum(best[r], jnp.maximum(s[:, 0:128], s[:, 128:256]))
            return carry

        lax.fori_loop(0, steps, score_step, 0)

        def top_step(g, carry):
            r = pl.ds(pl.multiple_of(g * 128, 128), 128)
            best[r] = jnp.broadcast_to(jnp.max(best[r], axis=1, keepdims=True), (128, 128))
            return carry

        lax.fori_loop(0, ROWS // 128, top_step, 0)

        def exp_step(j, carry):
            at = tile_at(j)
            for g in range(ROWS // 128):
                r = slice(g * 128, (g + 1) * 128)
                top = best[r]
                part = total[r]
                for half in range(TILE // 128):
                    lanes = pl.ds(pl.multiple_of(at + half * 128, 128), 128)
                    raised = jnp.exp2((scores[r, lanes] - top) * SCORE_EXP2)
                    scores[r, lanes] = raised
                    part = part + raised
                total[r] = part
            return carry

        lax.fori_loop(0, steps, exp_step, 0)

        def total_step(g, carry):
            r = pl.ds(pl.multiple_of(g * 128, 128), 128)
            whole = jnp.sum(total[r], axis=1, keepdims=True)
            total[r] = jnp.broadcast_to((1.0 / HM) / whole, (128, 128))
            return carry

        lax.fori_loop(0, ROWS // 128, total_step, 0)

        def index_logits(at):
            act = jnp.dot(
                qi_all[e], keys[704:832, pl.ds(at, TILE)], preferred_element_type=f32
            )
            out = jnp.zeros((GROUP, TILE), f32)
            for h in range(HI):
                r = slice(h * GROUP, (h + 1) * GROUP)
                w = w_all[e, r]
                out = out + jnp.maximum(act[r], 0.0) * jnp.concatenate([w, w], axis=1)
            return out

        def target_step(j, carry):
            at = tile_at(j)
            lanes = pl.ds(at, TILE)
            acc = jnp.zeros((GROUP, TILE), f32)
            for h in range(HM):
                r = slice(h * GROUP, (h + 1) * GROUP)
                share = total[r]
                acc = acc + scores[r, lanes] * jnp.concatenate([share, share], axis=1)
            target[:, lanes] = acc
            visible = key_pos(at, TILE) <= row_pos
            logits[:, lanes] = jnp.where(visible, index_logits(at), masked_value)
            return carry

        lax.fori_loop(0, steps, target_step, 0)

        masked = logits[...]
        visible = masked > 0.5 * masked_value
        top_logit = jnp.max(masked, axis=1, keepdims=True)
        lse = top_logit + jnp.log(jnp.sum(jnp.exp(masked - top_logit), axis=1, keepdims=True))
        loss = jnp.sum(jnp.where(visible, target[...] * (lse - masked), 0.0), axis=1, keepdims=True)
        rounded = jnp.where(visible, jnp.exp(masked - lse) - target[...], 0.0).astype(bf16)
        slope[...] = rounded.astype(f32)

        gsum[...] = jnp.zeros((IROWS, DI), f32)
        q_float = qi_all[e].astype(f32)
        weighted = jnp.transpose(q_float * w_all[e]).astype(bf16)

        def back_step(j, carry):
            at = tile_at(j)
            lanes = pl.ds(at, TILE)
            k = keys[704:832, lanes]
            act = jnp.dot(qi_all[e], k, preferred_element_type=f32)
            through = jnp.where(
                act.reshape(HI, GROUP, TILE) > 0.0, slope[:, lanes][None], 0.0
            ).reshape(IROWS, TILE).astype(bf16)
            gsum[...] += nt_dot(through, k)
            key_grad[:, lanes] += jnp.dot(weighted, through, preferred_element_type=f32)
            return carry

        lax.fori_loop(0, steps, back_step, 0)

        grads = (gsum[...] * w_all[e]).astype(bf16)
        column = jnp.sum(gsum[...] * q_float, axis=1, keepdims=True)
        lane = lax.broadcasted_iota(jnp.int32, (GROUP, 128), 1)
        high = loss.astype(bf16).astype(f32)
        middle = (loss - high).astype(bf16).astype(f32)
        low = loss - high - middle
        extra = jnp.where(lane == 8, high, jnp.where(lane == 9, middle, jnp.where(lane == 10, low, 0.0)))
        for dst in range(HEADS):
            small = extra
            for i in range(8):
                at = (dst * 8 + i) * GROUP
                to = KEY_ROWS + (e * 9 + i) * GROUP
                out_ref[dst, to : to + GROUP, :] = grads[at : at + GROUP]
                small = jnp.where(lane == i, column[at : at + GROUP], small)
            to = KEY_ROWS + (e * 9 + 8) * GROUP
            out_ref[dst, to : to + GROUP, :] = small.astype(bf16)

    def emit(i, carry):
        for late in range(2):
            lanes = pl.ds(pl.multiple_of(late * HALF + i * 128, 128), 128)
            turned = jnp.transpose(key_grad[:, lanes]).astype(bf16)
            for k in range(4):
                to = pl.multiple_of(i * 64 + (k // 2) * 32, 32)
                out_ref[2 * late + k % 2, pl.ds(to, 32), :] = turned[k * 32 : (k + 1) * 32]
        return carry

    lax.fori_loop(0, 16, emit, 0)


def rows_call(where, meta, gathered, queries):
    return pl.pallas_call(
        rows_kernel,
        out_shape=jax.ShapeDtypeStruct((HEADS, KEY_ROWS + GRAD_ROWS, DI), bf16),
        in_specs=[
            pl.BlockSpec(memory_space=pltpu.SMEM),
            pl.BlockSpec(memory_space=pltpu.SMEM),
            pl.BlockSpec(memory_space=pl.ANY),
            pl.BlockSpec(memory_space=pltpu.VMEM),
        ],
        out_specs=pl.BlockSpec(memory_space=pltpu.VMEM),
        scratch_shapes=[
            pltpu.VMEM((32, KW + DI, 128), bf16),
            pltpu.VMEM((832, LENGTH), bf16),
            pltpu.VMEM((2, 2, ROWS // 2, 640), bf16),
            pltpu.VMEM((2, IROWS, DI), bf16),
            pltpu.VMEM((ROWS, LENGTH), f32),
            pltpu.VMEM((ROWS, 128), f32),
            pltpu.VMEM((ROWS, 128), f32),
            pltpu.VMEM((2, IROWS, DI), f32),
            pltpu.VMEM((GROUP, LENGTH), f32),
            pltpu.VMEM((GROUP, LENGTH), f32),
            pltpu.VMEM((GROUP, LENGTH), f32),
            pltpu.VMEM((IROWS, DI), f32),
            pltpu.VMEM((DI, LENGTH), f32),
            pltpu.SemaphoreType.DMA((32,)),
        ],
        compiler_params=pltpu.CompilerParams(vmem_limit_bytes=58 * 1024 * 1024),
        name="rows_work",
    )(where, meta, gathered, queries)


def spread_kernel(to_ref, got_ref, out_ref, sums):
    total = got_ref[0, 0:KEY_ROWS].astype(f32)
    for src in range(1, HEADS):
        total = total + got_ref[src, 0:KEY_ROWS].astype(f32)
    sums[0:KEY_ROWS] = total.astype(bf16)
    sums[KEY_ROWS:] = jnp.zeros((32, DI), bf16)

    def put(d, carry):
        out_ref[d] = sums[pl.ds(pl.multiple_of(to_ref[d] * 32, 32), 32)]
        return carry

    lax.fori_loop(0, 64, put, 0, unroll=8)


def spread_call(to, got):
    return pl.pallas_call(
        spread_kernel,
        out_shape=jax.ShapeDtypeStruct((64, 32, DI), bf16),
        in_specs=[
            pl.BlockSpec(memory_space=pltpu.SMEM),
            pl.BlockSpec(memory_space=pltpu.VMEM),
        ],
        out_specs=pl.BlockSpec(memory_space=pltpu.VMEM),
        scratch_shapes=[pltpu.VMEM((KEY_ROWS + 32, DI), bf16)],
        name="spread_keys",
    )(to, got)


def body(block_order, main_query, latent_key, index_query, index_weight, index_key):
    d_own = lax.axis_index(CTX)
    early = block_order.reshape(64, 2)[:, 0]
    own = lax.dynamic_index_in_dim(early, d_own, 0, keepdims=False)
    first = own // 64 * 64
    c_own = own - first
    slots = lax.iota(jnp.int32, 64)
    wanted = first + lax.iota(jnp.int32, 32)
    where = jnp.sum(jnp.where(early[None, :] == wanted[:, None], slots[None, :], 0), axis=1)
    to = jnp.where(early // 64 * 64 == first, early - first, 32)
    meta = jnp.stack([c_own, lax.axis_index("head")]).astype(jnp.int32)

    shard = jnp.concatenate([latent_key, index_key], axis=0)
    gathered = gather_keys(shard)

    weights = jnp.pad(index_weight, ((0, 0), (0, 128 - index_weight.shape[1])))
    rows = jnp.concatenate([main_query, index_query.reshape(128, INDEX_LANES), weights], axis=1)
    rows = rows.reshape(2, HEADS, GROUP, ALL_LANES).swapaxes(0, 1)
    queries = lax.all_to_all(rows, "head", split_axis=0, concat_axis=0, tiled=True)

    sent = rows_call(where, meta, gathered, queries)
    got = lax.all_to_all(sent, "head", split_axis=0, concat_axis=0, tiled=True)
    parts = lax.all_to_all(spread_call(to, got), CTX, split_axis=0, concat_axis=0, tiled=True)
    grad_key = jnp.sum(parts.astype(f32), axis=0)

    grads = got[:, KEY_ROWS:].reshape(HEADS, 2, 9, GROUP, DI).transpose(1, 0, 3, 2, 4)
    grads = grads.reshape(128, 9, DI)
    small = grads[:, 8]
    row_loss = jnp.sum(small[:, 8:11].astype(f32), axis=1)
    return (row_loss, grads[:, 0:8], small[:, 0:8], grad_key)


def gather_keys(shard):
    return lax.all_gather(shard, CTX)


def solution(mesh):
    split = Mesh(
        mesh.devices.reshape(4, 8, 2, mesh.shape["head"]), ("ctx_0", "ctx_1", "ctx_2", "head")
    )
    in_specs = (
        P(),
        P(CTX, "head"),
        P(None, CTX),
        P(CTX, "head", None),
        P(CTX, "head"),
        P(None, CTX),
    )
    out_specs = (P(CTX), P(CTX, "head", None), P(CTX, "head"), P(CTX_HEAD, None))
    return jax.shard_map(body, mesh=split, in_specs=in_specs, out_specs=out_specs, check_vma=False)
```

time: 373 us -> 203 us (0.54); the launches traced: 366 us -> 201 us
  matrix products: 64.3 us -> 0 us
  other arithmetic: 68.7 us -> 8.28 us
  local copies, waits for them, and re-layouts: 56.6 us -> 6.28 us
  Pallas kernels: 0 us -> 44.5 us
  waiting for transfers between devices: 145 us -> 108 us
    reduce_scatter x4 -> x0, waiting for transfers between devices: 79.7 us -> none  [sum_in_order(): blocks = lax.psum_scatter(blocks, axes[k], scatter_dimension=0, tiled=True)]
    dot_general x20 -> x0, matrix products: 64.3 us -> none  [the longest x8 48.3 us: causal_target(): jnp.einsum('rhk,ks->hrs', grouped, window, preferred_element_type=jnp.flo...]
    div x8 -> x0, other arithmetic: 45.7 us -> none  [causal_target(): raised / jnp.sum(raised, axis=2, keepdims=True)]
    pallas_call x0 -> x2, Pallas kernels: none -> 44.5 us  [the longest x1 42.1 us: rows_call(): pl.pallas_call(rows_kernel, out_shape=jax.ShapeDtypeStruct((HEADS, KEY_RO...]
    all_to_all x4 -> x3, waiting for transfers between devices: 30.3 us -> 58.5 us  [the longest x1 27 us: body(): lax.all_to_all(rows, 'head', split_axis=0, concat_axis=0, tiled=True)]
    gather x3 -> x0, local copies, waits for them, and re-layouts: 18.3 us -> none  [the longest x1 12.2 us: body(): all_latent.reshape(key_width, block_total, block_rows)[:, slot_of, :]]
    all_gather x1, waiting for transfers between devices: 35.2 us -> 49.8 us  [gather_keys(): return lax.all_gather(shard, CTX)]
    split x5 -> x0, local copies, waits for them, and re-layouts: 13.2 us -> none  [the longest x2 11.7 us: side_by_side(): jnp.split(lax.all_gather(both, axis, axis=dim, tiled=True), ends, axis=al...]
  transfers between devices with their start and end apart: 9 -> 4, of which waited for: 7 -> 4; matrix products, arithmetic and copies ran while one was open for 10% -> 6% of each run, Pallas kernels for 0% -> 0%
where the time goes in v1:
time: 203 us; the launch traced here: 201 us
  waiting for transfers between devices  108 us (53%)
  Pallas kernels  44.5 us (22%)
  between operations  17.4 us (9%)
  starting transfers between devices  16.1 us (8%)
  other arithmetic  8.28 us (4%)
  local copies, waits for them, and re-layouts  6.28 us (3%)
    all_gather x1, waiting for transfers between devices, gather_keys(): return lax.all_gather(shard, CTX)  49.8 us
    pallas_call x1, Pallas kernels, rows_call(): pl.pallas_call(rows_kernel, out_shape=jax.ShapeDtypeStruct((HEADS, KEY_RO...  42.1 us
    all_to_all x1, waiting for transfers between devices, body(): lax.all_to_all(rows, 'head', split_axis=0, concat_axis=0, tiled=True)  27 us
    all_to_all x1, waiting for transfers between devices, body(): got = lax.all_to_all(sent, 'head', split_axis=0, concat_axis=0, tiled=True)  18.2 us
    all_to_all x1, waiting for transfers between devices, body(): lax.all_to_all(spread_call(to, got), CTX, split_axis=0, concat_axis=0, ti...  13.4 us
    all_to_all x1, starting transfers between devices, body(): lax.all_to_all(spread_call(to, got), CTX, split_axis=0, concat_axis=0, ti...  7.37 us
    all_to_all x1, starting transfers between devices, body(): lax.all_to_all(rows, 'head', split_axis=0, concat_axis=0, tiled=True)  4.42 us
    all_to_all x1, starting transfers between devices, body(): got = lax.all_to_all(sent, 'head', split_axis=0, concat_axis=0, tiled=True)  4.28 us
  transfers between devices with their start and end apart: 4, of which 4 were waited for; matrix products, arithmetic and copies ran while one was open for 6% of the time, Pallas kernels for 0%

profile of v1, /device:TPU:8, one launch (start us, length us, event | category | flops | bytes accessed | tf_op | source)
XLA Modules:
  0.0 200.9 jit_solution(4521170028260456292)
XLA Ops:
  7.2 0.0 all-gather.3.cloned.1.call-start
  7.2 1.6 pad_maximum_fusion.1
  8.8 0.0 all-gather.3.cloned.1.call-update
  8.8 1.1 concatenate.15
  9.9 0.8 copy.19
  10.7 3.5 %copy_bitcast_fusion = bf16[4,2,16,10368]{3,2,1,0:T(8,128)(2,1)} fusion(bf16[2,4,16,128]{3,2,1,0:T(8,128)(2,1)S(1)} %bitcast.21, bf16[2,4,16,1024]{3,2,1,0:T(8,128)(2,1)S(1)} %concatenate.15, bf16[2,4,16,9216]{3,2,1,0:T(8,128)(2,1)} %bitcast.16), kind=kLoop, calls=%fused_computation.1 | loop fusion | flops 7962624 | bytes 5308416 | tf_op jit(solution)/shard_map/transpose | solution.py:323
  14.2 0.0 copy-start.2
  14.2 4.4 %all-to-all-start = ((bf16[4,2,16,10368]{3,2,1,0:T(8,128)(2,1)}), bf16[4,2,16,10368]{3,2,1,0:T(8,128)(2,1)S(1)}, u32[]{:S(2)}, u32[]{:S(2)}) async-start(bf16[4,2,16,10368]{3,2,1,0:T(8,128)(2,1)} %copy_bitcast_fusion), calls=%async_computation | async-start | bytes 5308416 | tf_op jit(solution)/shard_map/all_to_all | solution.py:324
  18.6 0.0 copy-done.2
  18.6 0.1 reshape.30
  18.8 0.1 fusion
  18.9 0.5 constant_dynamic-slice_fusion
  22.7 0.6 pad_add_fusion.meta_ref
  23.3 0.7 select_reduce_fusion.where_ref
  23.9 27.0 %all-to-all-done.q_ref = bf16[4,2,16,10368]{3,2,1,0:T(8,128)(2,1)S(1)} async-done(((bf16[4,2,16,10368]{3,2,1,0:T(8,128)(2,1)}), bf16[4,2,16,10368]{3,2,1,0:T(8,128)(2,1)S(1)}, u32[]{:S(2)}, u32[]{:S(2)}) %all-to-all-start) | async-done | bytes 2654240 | tf_op jit(solution)/shard_map/all_to_all | solution.py:324
  50.9 0.0 copy-start
  50.9 49.8 %all-gather.3.cloned.1.call-done = bf16[45056,128]{1,0:T(8,128)(2,1)} async-done(((bf16[704,128]{1,0:T(8,128)(2,1)}), bf16[45056,128]{1,0:T(8,128)(2,1)}) %all-gather.3.cloned.1.call-update) | async-done | bytes 11534352 | tf_op jit(solution)/shard_map/all_gather | solution.py:339
  100.8 0.0 copy-done
  100.8 42.1 %rows_work.1 = bf16[4,1312,128]{2,1,0:T(8,128)(2,1)} custom-call(s32[32]{0:T(128)} %select_reduce_fusion.where_ref, s32[2]{0:T(128)} %pad_add_fusion.meta_ref, bf16[64,704,128]{2,1,0:T(8,128)(2,1)} %bitcast.15, bf16[4,2,16,10368]{3,2,1,0:T(8,128)(2,1)} %copy-done), custom_call_target="tpu_custom_call" | custom-call | tf_op jit(solution)/shard_map/rows_work/pallas_call | solution.py:247
  142.9 4.3 %all-to-all-start.1 = ((bf16[4,1312,128]{2,1,0:T(8,128)(2,1)}), bf16[4,1312,128]{2,1,0:T(8,128)(2,1)S(1)}, u32[]{:S(2)}, u32[]{:S(2)}) async-start(bf16[4,1312,128]{2,1,0:T(8,128)(2,1)} %rows_work.1), calls=%async_computation.1 | async-start | bytes 2686976 | tf_op jit(solution)/shard_map/all_to_all | solution.py:327
  147.2 0.5 compare_select_fusion.to_ref
  147.7 18.2 %all-to-all-done.1.got_ref = bf16[4,1312,128]{2,1,0:T(8,128)(2,1)S(1)} async-done(((bf16[4,1312,128]{2,1,0:T(8,128)(2,1)}), bf16[4,1312,128]{2,1,0:T(8,128)(2,1)S(1)}, u32[]{:S(2)}, u32[]{:S(2)}) %all-to-all-start.1) | async-done | bytes 1343520 | tf_op jit(solution)/shard_map/all_to_all | solution.py:327
  165.9 0.0 copy-start.1
  165.9 1.1 copy-done.1
  166.9 2.4 %spread_keys.1 = bf16[64,32,128]{2,1,0:T(8,128)(2,1)} custom-call(s32[64]{0:T(128)} %compare_select_fusion.to_ref, bf16[4,1312,128]{2,1,0:T(8,128)(2,1)} %copy-done.1), custom_call_target="tpu_custom_call" | custom-call | tf_op jit(solution)/shard_map/spread_keys/pallas_call | solution.py:293
  169.3 7.4 %all-to-all-start.2 = ((bf16[64,32,128]{2,1,0:T(8,128)(2,1)}), bf16[64,32,128]{2,1,0:T(8,128)(2,1)S(1)}, u32[]{:S(2)}, u32[]{:S(2)}) async-start(bf16[64,32,128]{2,1,0:T(8,128)(2,1)} %spread_keys.1), calls=%async_computation.2 | async-start | bytes 1048576 | tf_op jit(solution)/shard_map/all_to_all | solution.py:328
  176.7 1.0 slice.25
  177.8 0.9 copy.24
  178.7 0.7 copy.25
  179.3 0.7 convert_reduce_fusion.1
  180.0 13.4 %all-to-all-done.2 = bf16[64,32,128]{2,1,0:T(8,128)(2,1)S(1)} async-done(((bf16[64,32,128]{2,1,0:T(8,128)(2,1)}), bf16[64,32,128]{2,1,0:T(8,128)(2,1)S(1)}, u32[]{:S(2)}, u32[]{:S(2)}) %all-to-all-start.2) | async-done | bytes 524320 | tf_op jit(solution)/shard_map/all_to_all | solution.py:328
  193.4 0.7 convert_reduce_fusion
  (5 shorter events, 0.1 us)
Async XLA Ops:
  7.2 93.6 %all-gather.3.cloned.1.call-start = ((), (), s32[]{:S(2)}) async-start(), calls=%async_computation.3 | async-start | bytes 11714560 | tf_op jit(solution)/shard_map/all_gather | solution.py:339
  14.2 4.4 %copy-start.2 = (s32[128]{0:T(128)S(1)}, s32[128]{0:T(128)}, u32[]{:S(2)}) copy-start(s32[128]{0:T(128)} %param.6) | copy-start | bytes 1540
  14.2 36.7 %all-to-all-start = ((bf16[4,2,16,10368]{3,2,1,0:T(8,128)(2,1)}), bf16[4,2,16,10368]{3,2,1,0:T(8,128)(2,1)S(1)}, u32[]{:S(2)}, u32[]{:S(2)}) async-start(bf16[4,2,16,10368]{3,2,1,0:T(8,128)(2,1)} %copy_bitcast_fusion), calls=%async_computation | async-start | bytes 5308416 | tf_op jit(solution)/shard_map/all_to_all | solution.py:324
  50.9 49.8 %copy-start = (bf16[4,2,16,10368]{3,2,1,0:T(8,128)(2,1)}, bf16[4,2,16,10368]{3,2,1,0:T(8,128)(2,1)S(1)}, u32[]{:S(2)}) copy-start(bf16[4,2,16,10368]{3,2,1,0:T(8,128)(2,1)S(1)} %all-to-all-done.q_ref) | copy-start | bytes 7962628
  142.9 23.0 %all-to-all-start.1 = ((bf16[4,1312,128]{2,1,0:T(8,128)(2,1)}), bf16[4,1312,128]{2,1,0:T(8,128)(2,1)S(1)}, u32[]{:S(2)}, u32[]{:S(2)}) async-start(bf16[4,1312,128]{2,1,0:T(8,128)(2,1)} %rows_work.1), calls=%async_computation.1 | async-start | bytes 2686976 | tf_op jit(solution)/shard_map/all_to_all | solution.py:327
  165.9 1.1 copy-start.1
  169.3 24.0 %all-to-all-start.2 = ((bf16[64,32,128]{2,1,0:T(8,128)(2,1)}), bf16[64,32,128]{2,1,0:T(8,128)(2,1)S(1)}, u32[]{:S(2)}, u32[]{:S(2)}) async-start(bf16[64,32,128]{2,1,0:T(8,128)(2,1)} %spread_keys.1), calls=%async_computation.2 | async-start | bytes 1048576 | tf_op jit(solution)/shard_map/all_to_all | solution.py:328
Sparse Core Ops, SparseCore 0:
  11.3 89.4 all-gather.2
